TPU v7x, 32 devices: a whole 2x2x4 slice. The times are simulated.
32 devices in a mesh: member: 2 (over x), lat: 16 (over z, y, core).
Axes of the slice: x: 2, y: 2, z: 4, core: 2. Of those that a mesh axis runs over, the one named last changes fastest.
Arguments:
- height: float32 [128, 32, 1440], P(('member', 'lat')), parts along dimension 0, may hold values from -6 to 6
- zonal_courant: float32 [128, 32, 1440], P(('member', 'lat')), parts along dimension 0, may hold values from -1.5 to 1.5
- merid_courant: float32 [128, 32, 1440], P(('member', 'lat')), parts along dimension 0, may hold values from -1.5 to 1.5
- rates: float32 [64], P('member'), parts along dimension 0, may hold values from 0.05 to 0.5
- thresholds: float32 [64], P('member'), parts along dimension 0, may hold values from -3 to 3
- flags: int32 [64], replicated, may hold values from 0 to 1, as said below
- cutoffs: int32 [64], replicated, may hold values from 45 to 360
Outputs:
- filtered_height: float32 [128, 32, 1440], P(('member', 'lat')), parts along dimension 0
There are 2 independent parts, one for each index of `member`. A program takes and returns all parts, laid end to end along the dimension named above; an argument that names none is the same for every part. Nothing has to cross between parts.
Inputs may be any that keep to these rules, and one draw needn't show every extreme that they name: flags is 1 on a southern band of rows that starts at row 0 and on a northern band that ends at row 63, each band 64 // 8 to 16 rows long, and 0 on all other rows.
All inputs are finite; a program needn't handle non-finite values.
Results may differ from a plain program's by a relative error of at most 0.00007.
Values sent between devices are 32-bit elements; how exact they have to be, the bound alone decides.
No kernel may reach another device: no remote copies, remote signals or barrier semaphores. Data moves between devices by JAX's collectives and lax.ppermute only.
A program may use at most 64 MiB of HBM per device.

v0:
```python
import jax
import jax.numpy as jnp
from jax import lax
from jax.sharding import PartitionSpec as P


def padded_2(cells, sides, width):
    for axis, dim in sides:
        count = lax.axis_size(axis)
        ends = count - 1
        head = lax.slice_in_dim(cells, 0, width, axis=dim)
        tail = lax.slice_in_dim(cells, cells.shape[dim] - width, cells.shape[dim], axis=dim)
        cells = jnp.concatenate(
            [
                lax.ppermute(tail, axis, [(i, (i + 1) % count) for i in range(ends)]),
                cells,
                lax.ppermute(head, axis, [((i + 1) % count, i) for i in range(ends)]),
            ],
            axis=dim,
        )
    return cells


def transform_table(nlon, nkp):
    points = jnp.arange(nlon, dtype=jnp.int32)
    waves = jnp.arange(nkp, dtype=jnp.int32)
    phase = points[:, None] * waves[None, :] % nlon
    angle = 2.0 * jnp.pi / nlon * phase.astype(jnp.float32)
    return jnp.concatenate([jnp.cos(angle), jnp.sin(angle)], axis=1)


def wave_weights(nlon, nkp):
    waves = jnp.arange(nkp, dtype=jnp.int32)
    interior = jnp.where((waves > 0) & (waves < nlon // 2), 2.0, 1.0)
    return jnp.where(waves <= nlon // 2, interior, 0.0).astype(jnp.float32) / nlon


def damping(row_flags, row_cutoffs, nkp):
    waves = jnp.maximum(jnp.arange(nkp), 1).astype(jnp.float32)
    ratio = row_cutoffs.astype(jnp.float32)[:, None] / waves[None, :]
    factor = jnp.minimum(1.0, ratio * ratio)
    return jnp.where(row_flags[:, None] > 0, factor, 1.0)


def filter_units(flat, damp, table, weights):
    highest = lax.Precision.HIGHEST
    spectrum = jnp.dot(flat, table, precision=highest, preferred_element_type=jnp.float32)
    factor = (1.0 - damp) * weights[None, :]
    scaled = spectrum * jnp.concatenate([factor, factor], axis=1)
    dims = (((1,), (1,)), ((), ()))
    removed = lax.dot_general(
        scaled, table, dims, precision=highest, preferred_element_type=jnp.float32
    )
    return flat - removed


def filtered_or_kept(block, row_flags, row_cutoffs, table, weights):
    rows, levels, nlon = block.shape
    damp = damping(row_flags, row_cutoffs, weights.shape[0])
    unit_damp = jnp.broadcast_to(damp[:, None, :], (rows, levels, damp.shape[1])).reshape(
        rows * levels, damp.shape[1]
    )

    def apply_filter(data):
        return filter_units(data.reshape(rows * levels, nlon), unit_damp, table, weights).reshape(
            rows, levels, nlon
        )

    def keep_block(data):
        return data

    return lax.cond(jnp.any(row_flags > 0), apply_filter, keep_block, block)


def face_fluxes(rows_height, rows_speed, face_cos, count):
    face_value = (
        7.0 * (rows_height[1 : count + 1] + rows_height[2 : count + 2])
        - (rows_height[0:count] + rows_height[3 : count + 3])
    ) / 12.0
    speed = 0.5 * (rows_speed[0:count] + rows_speed[1 : count + 1]) * face_cos[:, None, None]
    return speed * face_value


def face_cosines(face_ids, nlat):
    return jnp.where(
        (face_ids > 0) & (face_ids < nlat),
        jnp.sin(jnp.pi * face_ids.astype(jnp.float32) / nlat),
        jnp.float32(0.0),
    )


def local(height, zonal_courant, merid_courant, rates, thresholds, flags, cutoffs):
    lat_rows, levels, nlon = height.shape
    devices = lax.axis_size("lat")
    position = lax.axis_index("lat")
    first_row = position * lat_rows
    nlat = lat_rows * devices
    local_rows = first_row + jnp.arange(lat_rows, dtype=jnp.int32)
    cos_rows = jnp.sin(jnp.pi * (local_rows.astype(jnp.float32) + 0.5) / nlat)
    faces = first_row + jnp.arange(lat_rows + 1, dtype=jnp.int32)
    cos_faces = face_cosines(faces, nlat)
    padded = padded_2(jnp.stack([height, merid_courant]), (("lat", 1),), 2)
    east = jnp.roll(height, -1, axis=2)
    west = jnp.roll(height, 1, axis=2)
    far_east = jnp.roll(height, -2, axis=2)
    face_height = (7.0 * (height + east) - (west + far_east)) / 12.0
    face_speed = 0.5 * (zonal_courant + jnp.roll(zonal_courant, -1, axis=2))
    zonal_flux = face_speed * face_height
    zonal_div = zonal_flux - jnp.roll(zonal_flux, 1, axis=2)
    source = -rates[None, :, None] * jax.nn.softplus(height - thresholds[None, :, None])
    partial_sums = jnp.sum(jnp.sum(source, axis=2) * cos_rows[:, None], axis=0)
    totals = lax.psum(partial_sums, "lat")
    all_rows = jnp.arange(nlat, dtype=jnp.int32)
    area = nlon * jnp.sum(jnp.sin(jnp.pi * (all_rows.astype(jnp.float32) + 0.5) / nlat))
    level_mean = totals / area
    padded_height = padded[0]
    padded_speed = padded[1]
    count = lat_rows + 1
    merid_flux = face_fluxes(padded_height, padded_speed[1:], cos_faces, count)
    merid_div = (merid_flux[1:] - merid_flux[:-1]) / cos_rows[:, None, None]
    updated = height - zonal_div - merid_div + source - level_mean[None, :, None]
    nkp = (nlon // 2 + 128) // 128 * 128
    table = transform_table(nlon, nkp)
    weights = wave_weights(nlon, nkp)
    row_flags = lax.dynamic_slice_in_dim(flags, first_row, lat_rows)
    row_cutoffs = lax.dynamic_slice_in_dim(cutoffs, first_row, lat_rows)
    result = filtered_or_kept(updated, row_flags, row_cutoffs, table, weights)
    return result


def solution(mesh):
    return jax.shard_map(
        local,
        mesh=mesh,
        in_specs=(
            P(("member", "lat"), None, None),
            P(("member", "lat"), None, None),
            P(("member", "lat"), None, None),
            P("member"),
            P("member"),
            P(),
            P(),
        ),
        out_specs=P(("member", "lat"), None, None),
        check_vma=False,
    )
```

profile of v0, /device:TPU:0, one launch (start us, length us, event | category | flops | bytes accessed | tf_op | source)
XLA Modules:
  0.0 101.5 jit_solution(3019089762479028692)
XLA Ops:
  0.0 2.8 %fusion.17 = (f32[2,2,32,1440]{3,2,1,0:T(8,128)}, f32[2,2,32,1440]{3,2,1,0:T(8,128)}) fusion(f32[1,4,32,1440]{3,2,1,0:T(8,128)} %bitcast.21, f32[1,4,32,1440]{3,2,1,0:T(8,128)} %bitcast.27), kind=kLoop, calls=%fused_computation.33 | loop fusion | flops 368640 | bytes 2949120 | tf_op jit(solution)/shard_map/stack | solution.py:102
  2.8 3.3 %collective-permute-start = (f32[2,2,32,1440]{3,2,1,0:T(8,128)}, f32[2,2,32,1440]{3,2,1,0:T(8,128)}, u32[]{:S(2)}, u32[]{:S(2)}) collective-permute-start(f32[2,2,32,1440]{3,2,1,0:T(8,128)} %get-tuple-element.115), channel_id=1, source_target_pairs={{0,1},{1,2},{2,3},{3,4},{4,5},{5,6},{6,7},{7,8},{8,9},{9,10},{10,1... | collective-permute-start | bytes 2211848 | tf_op jit(solution)/shard_map/ppermute | solution.py:15
  6.1 1.3 %collective-permute-start.1 = (f32[2,2,32,1440]{3,2,1,0:T(8,128)}, f32[2,2,32,1440]{3,2,1,0:T(8,128)}, u32[]{:S(2)}, u32[]{:S(2)}) collective-permute-start(f32[2,2,32,1440]{3,2,1,0:T(8,128)} %get-tuple-element.116), channel_id=1, source_target_pairs={{1,0},{2,1},{3,2},{4,3},{5,4},{6,5},{7,6},{8,7},{9,8},{10,9},{11,1... | collective-permute-start | bytes 2211848 | tf_op jit(solution)/shard_map/ppermute | solution.py:17
  7.3 2.8 %fusion.33 = (f32[4,32,1439]{2,1,0:T(8,128)}, f32[4,32,1439]{2,1,0:T(8,128)}) fusion(f32[4,32,1440]{2,1,0:T(8,128)} %param.9), kind=kLoop, calls=%fused_computation.63 | loop fusion | bytes 2947072 | tf_op jit(solution)/shard_map/jit(_roll_static)/slice | solution.py:104
  10.1 0.1 fusion.32
  10.2 0.3 slice.95
  10.5 1.2 %slice.89 = f32[4,32,1439]{2,1,0:T(8,128)} slice(f32[4,32,1440]{2,1,0:T(8,128)S(1)} %copy-done.2), slice={[0:4], [0:32], [1:1440]} | slice | bytes 1473536 | tf_op jit(solution)/shard_map/jit(_roll_static)/slice | solution.py:107
  11.8 0.7 sine_reduce_fusion
  12.5 19.6 %fusion.7 = (f32[1440,768]{1,0:T(8,128)}, f32[1440,768]{1,0:T(8,128)}) fusion(), kind=kLoop, calls=%fused_computation.15 | loop fusion | flops 9953280 | bytes 8847360 | tf_op jit(solution)/shard_map/sin | solution.py:29
  32.1 0.9 fusion.29
  33.0 0.1 multiply_reduce_fusion
  33.1 35.8 %psum.7 = f32[32]{0:T(128)S(1)} all-reduce(f32[32]{0:T(128)S(1)} %multiply_reduce_fusion), channel_id=1, replica_groups=mesh['member'=2,'lat'=16] {'lat'}, use_global_device_ids=true, to_apply=%region_3.4 | all-reduce | flops 32 | bytes 256 | tf_op jit(solution)/shard_map/psum | solution.py:112
  68.9 0.1 slice.109
  69.0 0.8 fusion.31
  71.2 8.2 %pad_maximum_fusion = f32[1440,1536]{1,0:T(8,128)} fusion(f32[1440,768]{1,0:T(8,128)} %get-tuple-element.123, f32[1440,768]{1,0:T(8,128)} %get-tuple-element.124), kind=kLoop, calls=%fused_computation.8 | loop fusion | flops 2211840 | bytes 17694720 | tf_op jit(solution)/shard_map/concatenate | solution.py:29
  79.4 1.9 %maximum_maximum_fusion = (f32[2,6,32,1440]{3,2,1,0:T(8,128)S(1)}, f32[2,6,32,1440]{3,2,1,0:T(8,128)S(1)}) fusion(f32[1,4,32,1440]{3,2,1,0:T(8,128)S(1)} %bitcast.28, f32[1,4,32,1440]{3,2,1,0:T(8,128)S(1)} %bitcast.22, f32[2,2,32,1440]{3,2,1,0:T(8,128)} %collective-permute-done, f32[2,2,32,1440]{3,2,1,0:T(8,128)} %collective-permute-done.1), kind=kLoop, calls=%fused_computation.18 | loop fusion | flops 2211840 | bytes 7372800 | tf_op jit(solution)/shard_map/concatenate | solution.py:13
  81.3 0.5 fusion.13
  81.8 0.7 fusion.22
  82.6 18.0 %conditional.1 = (f32[4,32,1440]{2,1,0:T(8,128)S(1)}) conditional(s32[]{:T(128)} %convert_element_type.42, f32[4,32,1440]{2,1,0:T(8,128)S(1)} %fusion.22, (f32[4,32,1440]{2,1,0:T(8,128)S(1)}, f32[1440,1536]{1,0:T(8,128)}, pred[4]{0:T(512)(128)(4,1)S(1)}, f32[4]{0:T(128)S(1)}, f32[1,768]{1,0:T(1,128)S(1)}, /*index=5*/s32[768]{0:T(1024)S(1)}) %tuple.45), branch_computations={%region_5.6_spmd, %region_6.7_spmd} | conditional | flops 6795468800 | bytes 25258016 | solution.py:72
  82.9 7.6 %convolution_multiply_fusion = f32[128,1536]{1,0:T(8,128)S(1)} fusion(f32[128,1440]{1,0:T(8,128)S(1)} %bitcast.24, f32[1440,1536]{1,0:T(8,128)} %get-tuple-element.105, f32[128,768]{1,0:T(8,128)S(1)} %bitcast_multiply_fusion), kind=kOutput, calls=%fused_computation.1 | convolution fusion | flops 3397779456 | bytes 10764288 | tf_op jit(solution)/shard_map/cond/branch_1_fun/dot_general | solution.py:47
  90.6 0.3 copy.27
  90.8 9.5 %convolution_subtract_fusion = f32[128,1440]{0,1:T(8,128)S(1)} fusion(f32[128,1440]{0,1:T(8,128)S(1)} %copy.27, f32[128,1536]{1,0:T(8,128)S(1)} %convolution_multiply_fusion, f32[1440,1536]{1,0:T(8,128)} %get-tuple-element.105), kind=kOutput, calls=%fused_computation | convolution fusion | flops 3397570560 | bytes 11108352 | tf_op jit(solution)/shard_map/cond/branch_1_fun/dot_general | solution.py:51
  100.3 0.3 copy.28
  100.6 0.9 copy-done.1
  (37 shorter events, 0.4 us)
Async XLA Ops:
  0.0 10.1 %copy-start = (f32[4,32,1440]{2,1,0:T(8,128)S(1)}, f32[4,32,1440]{2,1,0:T(8,128)}, u32[]{:S(2)}) copy-start(f32[4,32,1440]{2,1,0:T(8,128)} %param.9) | copy-start | bytes 2211844
  0.0 10.5 %copy-start.2 = (f32[4,32,1440]{2,1,0:T(8,128)S(1)}, f32[4,32,1440]{2,1,0:T(8,128)}, u32[]{:S(2)}) copy-start(f32[4,32,1440]{2,1,0:T(8,128)} %param.10) | copy-start | bytes 2211844
  2.8 76.6 %collective-permute-start = (f32[2,2,32,1440]{3,2,1,0:T(8,128)}, f32[2,2,32,1440]{3,2,1,0:T(8,128)}, u32[]{:S(2)}, u32[]{:S(2)}) collective-permute-start(f32[2,2,32,1440]{3,2,1,0:T(8,128)} %get-tuple-element.115), channel_id=1, source_target_pairs={{0,1},{1,2},{2,3},{3,4},{4,5},{5,6},{6,7},{7,8},{8,9},{9,10},{10,1... | collective-permute-start | bytes 2211848 | tf_op jit(solution)/shard_map/ppermute | solution.py:15
  6.1 73.3 %collective-permute-start.1 = (f32[2,2,32,1440]{3,2,1,0:T(8,128)}, f32[2,2,32,1440]{3,2,1,0:T(8,128)}, u32[]{:S(2)}, u32[]{:S(2)}) collective-permute-start(f32[2,2,32,1440]{3,2,1,0:T(8,128)} %get-tuple-element.116), channel_id=1, source_target_pairs={{1,0},{2,1},{3,2},{4,3},{5,4},{6,5},{7,6},{8,7},{9,8},{10,9},{11,1... | collective-permute-start | bytes 2211848 | tf_op jit(solution)/shard_map/ppermute | solution.py:17
  12.4 19.6 %copy-start.9 = (f32[32]{0:T(128)S(1)}, f32[32]{0:T(128)}, u32[]{:S(2)}) copy-start(f32[32]{0:T(128)} %param.12) | copy-start | bytes 388
  12.4 19.6 %slice-start = ((f32[4,32,1440]{2,1,0:T(8,128)}), f32[4,32,1]{2,1,0:T(8,128)S(1)}, s32[]{:S(2)}) async-start(f32[4,32,1440]{2,1,0:T(8,128)} %param.10), calls=%async_computation | async-start | bytes 131072 | tf_op jit(solution)/shard_map/jit(_roll_static)/slice | solution.py:107
  12.4 19.7 %copy-start.3 = (f32[4,32,1439]{2,1,0:T(8,128)S(1)}, f32[4,32,1439]{2,1,0:T(8,128)}, u32[]{:S(2)}) copy-start(f32[4,32,1439]{2,1,0:T(8,128)} %slice.89) | copy-start | bytes 2210308
  12.4 19.7 %copy-start.4 = (f32[4,32,1439]{2,1,0:T(8,128)S(1)}, f32[4,32,1439]{2,1,0:T(8,128)}, u32[]{:S(2)}) copy-start(f32[4,32,1439]{2,1,0:T(8,128)} %get-tuple-element.121) | copy-start | bytes 2210308
  12.4 19.7 %copy-start.5 = (f32[4,32,1439]{2,1,0:T(8,128)S(1)}, f32[4,32,1439]{2,1,0:T(8,128)}, u32[]{:S(2)}) copy-start(f32[4,32,1439]{2,1,0:T(8,128)} %get-tuple-element.122) | copy-start | bytes 2210308
  12.4 19.7 %copy-start.7 = (f32[32]{0:T(128)S(1)}, f32[32]{0:T(128)}, u32[]{:S(2)}) copy-start(f32[32]{0:T(128)} %param.13) | copy-start | bytes 388
  32.0 37.0 %copy-start.8 = (s32[64]{0:T(128)S(1)}, s32[64]{0:T(128)}, u32[]{:S(2)}) copy-start(s32[64]{0:T(128)} %param.14) | copy-start | bytes 772
  32.0 37.8 %copy-start.10 = (s32[64]{0:T(128)S(1)}, s32[64]{0:T(128)}, u32[]{:S(2)}) copy-start(s32[64]{0:T(128)} %param.15) | copy-start | bytes 772
  71.2 8.2 %copy-start.6 = (f32[4,32,1440]{2,1,0:T(8,128)S(1)}, f32[4,32,1440]{2,1,0:T(8,128)}, u32[]{:S(2)}) copy-start(f32[4,32,1440]{2,1,0:T(8,128)} %param.11) | copy-start | bytes 2211844
  100.6 0.9 copy-start.1
where the time goes:
time: 102 us; the launch traced here: 101 us
  other arithmetic  36.4 us (36%)
  blocking collectives  35.8 us (35%)
  matrix products  17.1 us (17%)
  local copies, waits for them, and re-layouts  5.82 us (6%)
  starting transfers between devices  4.55 us (4%)
  between operations  1.52 us (1%)
    psum x1, blocking collectives, local(): totals = lax.psum(partial_sums, 'lat')  35.8 us
    sin x1, other arithmetic, transform_table(): return jnp.concatenate([jnp.cos(angle), jnp.sin(angle)], axis=1)  19.6 us
    dot_general x1, matrix products, filter_units(): lax.dot_general(scaled, table, dims, precision=highest, preferred_element...  9.48 us
    concatenate x1, other arithmetic, transform_table(): return jnp.concatenate([jnp.cos(angle), jnp.sin(angle)], axis=1)  8.16 us
    dot_general x1, matrix products, filter_units(): jnp.dot(flat, table, precision=highest, preferred_element_type=jnp.float32)  7.64 us
    ppermute x1, starting transfers between devices, padded_2(): lax.ppermute(tail, axis, [(i, (i + 1) % count) for i in range(ends)])  3.27 us
    slice x2, local copies, waits for them, and re-layouts, local(): west = jnp.roll(height, 1, axis=2)  2.85 us
    another operation x1, other arithmetic, local(): padded = padded_2(jnp.stack([height, merid_courant]), (('lat', 1),), 2)  2.78 us
  transfers between devices with their start and end apart: 2, of which 0 were waited for; matrix products, arithmetic and copies ran while one was open for 34% of the time, Pallas kernels for 0%

commit v1 on v0

--- a/solution.py
+++ b/solution.py
@@ -109,7 +109,7 @@
     zonal_div = zonal_flux - jnp.roll(zonal_flux, 1, axis=2)
     source = -rates[None, :, None] * jax.nn.softplus(height - thresholds[None, :, None])
     partial_sums = jnp.sum(jnp.sum(source, axis=2) * cos_rows[:, None], axis=0)
-    totals = lax.psum(partial_sums, "lat")
+    totals = jnp.sum(lax.all_gather(partial_sums, "lat"), axis=0)
     all_rows = jnp.arange(nlat, dtype=jnp.int32)
     area = nlon * jnp.sum(jnp.sin(jnp.pi * (all_rows.astype(jnp.float32) + 0.5) / nlat))
     level_mean = totals / area

time: 102 us -> 105 us (1.029)
  other arithmetic: 36.4 us -> 38 us
  local copies, waits for them, and re-layouts: 5.82 us -> 6.91 us
    unnamed x0 -> x1, blocking collectives: none -> 35.8 us
    psum x1 -> x0, blocking collectives: 35.8 us -> none  [local(): totals = lax.psum(partial_sums, 'lat')]
    reduce_sum x2, other arithmetic: 1 us -> 2.59 us  [local(): partial_sums = jnp.sum(jnp.sum(source, axis=2) * cos_rows[:, None], axis=0)]
  transfers between devices with their start and end apart: 2 -> 2, of which waited for: 0 -> 0; matrix products, arithmetic and copies ran while one was open for 34% -> 36% of each run, Pallas kernels for 0% -> 0%
where the time goes in v1:
time: 105 us
  other arithmetic  38 us (36%)
  blocking collectives  35.8 us (34%)
  matrix products  17.1 us (16%)
  local copies, waits for them, and re-layouts  6.91 us (7%)
  starting transfers between devices  4.54 us (4%)
  between operations  2.04 us (2%)
    unnamed x1, blocking collectives  35.8 us
    sin x1, other arithmetic, transform_table(): return jnp.concatenate([jnp.cos(angle), jnp.sin(angle)], axis=1)  19.5 us
    dot_general x1, matrix products, filter_units(): lax.dot_general(scaled, table, dims, precision=highest, preferred_element...  9.48 us
    concatenate x1, other arithmetic, transform_table(): return jnp.concatenate([jnp.cos(angle), jnp.sin(angle)], axis=1)  8.16 us
    dot_general x1, matrix products, filter_units(): jnp.dot(flat, table, precision=highest, preferred_element_type=jnp.float32)  7.63 us
    ppermute x1, starting transfers between devices, padded_2(): lax.ppermute(tail, axis, [(i, (i + 1) % count) for i in range(ends)])  3.26 us
    slice x2, local copies, waits for them, and re-layouts, local(): west = jnp.roll(height, 1, axis=2)  2.97 us
    another operation x1, other arithmetic, local(): padded = padded_2(jnp.stack([height, merid_courant]), (('lat', 1),), 2)  2.77 us
  transfers between devices with their start and end apart: 2, of which 0 were waited for; matrix products, arithmetic and copies ran while one was open for 36% of the time, Pallas kernels for 0%

profile of v1, /device:TPU:0, one launch (start us, length us, event | category | flops | bytes accessed | tf_op | source)
XLA Modules:
  0.0 104.6 jit_solution(9163502437678456586)
XLA Ops:
  0.0 2.8 %fusion.17 = (f32[2,2,32,1440]{3,2,1,0:T(8,128)}, f32[2,2,32,1440]{3,2,1,0:T(8,128)}) fusion(f32[1,4,32,1440]{3,2,1,0:T(8,128)} %bitcast.22, f32[1,4,32,1440]{3,2,1,0:T(8,128)} %bitcast.28), kind=kLoop, calls=%fused_computation.33 | loop fusion | flops 368640 | bytes 2949120 | tf_op jit(solution)/shard_map/stack | solution.py:102
  2.8 3.3 %collective-permute-start = (f32[2,2,32,1440]{3,2,1,0:T(8,128)}, f32[2,2,32,1440]{3,2,1,0:T(8,128)}, u32[]{:S(2)}, u32[]{:S(2)}) collective-permute-start(f32[2,2,32,1440]{3,2,1,0:T(8,128)} %get-tuple-element.115), channel_id=1, source_target_pairs={{0,1},{1,2},{2,3},{3,4},{4,5},{5,6},{6,7},{7,8},{8,9},{9,10},{10,1... | collective-permute-start | bytes 2211848 | tf_op jit(solution)/shard_map/ppermute | solution.py:15
  6.0 1.3 %collective-permute-start.1 = (f32[2,2,32,1440]{3,2,1,0:T(8,128)}, f32[2,2,32,1440]{3,2,1,0:T(8,128)}, u32[]{:S(2)}, u32[]{:S(2)}) collective-permute-start(f32[2,2,32,1440]{3,2,1,0:T(8,128)} %get-tuple-element.116), channel_id=1, source_target_pairs={{1,0},{2,1},{3,2},{4,3},{5,4},{6,5},{7,6},{8,7},{9,8},{10,9},{11,1... | collective-permute-start | bytes 2211848 | tf_op jit(solution)/shard_map/ppermute | solution.py:17
  7.3 2.9 %fusion.33 = (f32[4,32,1439]{2,1,0:T(8,128)}, f32[4,32,1439]{2,1,0:T(8,128)}) fusion(f32[4,32,1440]{2,1,0:T(8,128)} %param.9), kind=kLoop, calls=%fused_computation.63 | loop fusion | bytes 2947072 | tf_op jit(solution)/shard_map/jit(_roll_static)/slice | solution.py:104
  10.3 0.3 slice.95
  10.6 1.2 %slice.89 = f32[4,32,1439]{2,1,0:T(8,128)} slice(f32[4,32,1440]{2,1,0:T(8,128)S(1)} %copy-done.2), slice={[0:4], [0:32], [1:1440]} | slice | bytes 1473536 | tf_op jit(solution)/shard_map/jit(_roll_static)/slice | solution.py:107
  11.9 0.6 sine_reduce_fusion
  12.5 19.5 %fusion.7 = (f32[1440,768]{1,0:T(8,128)}, f32[1440,768]{1,0:T(8,128)}) fusion(), kind=kLoop, calls=%fused_computation.15 | loop fusion | flops 9953280 | bytes 8847360 | tf_op jit(solution)/shard_map/sin | solution.py:29
  32.1 2.5 %fusion.29 = (f32[4,32]{1,0:T(4,128)S(1)}, f32[4,32,1440]{2,1,0:T(8,128)S(1)}) fusion(f32[4,32,1440]{2,1,0:T(8,128)S(1)} %copy-done, f32[32]{0:T(128)S(1)} %copy-done.5, f32[32]{0:T(128)S(1)} %neg.8, f32[4,32,2]{2,1,0:T(8,128)S(1)} %slice.96, f32[4,32,1438]{2,1,0:T(8,128)S(1)} %slice.95, f32[4,32,1439]{2,1,0:T(8,128)} %get-tuple-element.121, ...), kind=kLoop, calls=%fused_computation.51 | loop fusion | flops 3870592 | bytes 5161728 | tf_op jit(solution)/shard_map/reduce_sum | solution.py:111
  34.7 0.1 multiply_reduce_fusion
  34.7 0.6 dynamic-slice
  36.0 0.2 dynamic-update-slice
  36.3 35.8 %all-reduce = f32[512]{0:T(512)S(1)} all-reduce(f32[512]{0:T(512)S(1)} %dynamic-update-slice), channel_id=2, replica_groups=mesh['member'=2,'lat'=16] {'lat'}, use_global_device_ids=true, to_apply=%add | all-reduce | flops 512 | bytes 4096
  72.3 0.8 fusion.31
  74.3 8.2 %pad_maximum_fusion = f32[1440,1536]{1,0:T(8,128)} fusion(f32[1440,768]{1,0:T(8,128)} %get-tuple-element.123, f32[1440,768]{1,0:T(8,128)} %get-tuple-element.124), kind=kLoop, calls=%fused_computation.8 | loop fusion | flops 2211840 | bytes 17694720 | tf_op jit(solution)/shard_map/concatenate | solution.py:29
  82.5 1.9 %maximum_maximum_fusion = (f32[2,6,32,1440]{3,2,1,0:T(8,128)S(1)}, f32[2,6,32,1440]{3,2,1,0:T(8,128)S(1)}) fusion(f32[1,4,32,1440]{3,2,1,0:T(8,128)S(1)} %bitcast.29, f32[1,4,32,1440]{3,2,1,0:T(8,128)S(1)} %bitcast.23, f32[2,2,32,1440]{3,2,1,0:T(8,128)} %collective-permute-done, f32[2,2,32,1440]{3,2,1,0:T(8,128)} %collective-permute-done.1), kind=kLoop, calls=%fused_computation.18 | loop fusion | flops 2211840 | bytes 7372800 | tf_op jit(solution)/shard_map/concatenate | solution.py:13
  84.5 0.5 fusion.13
  85.0 0.7 fusion.22
  85.7 18.0 %conditional.1 = (f32[4,32,1440]{2,1,0:T(8,128)S(1)}) conditional(s32[]{:T(128)} %convert_element_type.42, f32[4,32,1440]{2,1,0:T(8,128)S(1)} %fusion.22, (f32[4,32,1440]{2,1,0:T(8,128)S(1)}, f32[1440,1536]{1,0:T(8,128)}, pred[4]{0:T(512)(128)(4,1)S(1)}, f32[4]{0:T(128)S(1)}, f32[1,768]{1,0:T(1,128)S(1)}, /*index=5*/s32[768]{0:T(1024)S(1)}) %tuple.45), branch_computations={%region_5.6_spmd, %region_6.7_spmd} | conditional | flops 6795468800 | bytes 25258016 | solution.py:72
  86.1 7.6 %convolution_multiply_fusion = f32[128,1536]{1,0:T(8,128)S(1)} fusion(f32[128,1440]{1,0:T(8,128)S(1)} %bitcast.25, f32[1440,1536]{1,0:T(8,128)} %get-tuple-element.105, f32[128,768]{1,0:T(8,128)S(1)} %bitcast_multiply_fusion), kind=kOutput, calls=%fused_computation.1 | convolution fusion | flops 3397779456 | bytes 10764288 | tf_op jit(solution)/shard_map/cond/branch_1_fun/dot_general | solution.py:47
  93.7 0.3 copy.27
  94.0 9.5 %convolution_subtract_fusion = f32[128,1440]{0,1:T(8,128)S(1)} fusion(f32[128,1440]{0,1:T(8,128)S(1)} %copy.27, f32[128,1536]{1,0:T(8,128)S(1)} %convolution_multiply_fusion, f32[1440,1536]{1,0:T(8,128)} %get-tuple-element.105), kind=kOutput, calls=%fused_computation | convolution fusion | flops 3397570560 | bytes 11108352 | tf_op jit(solution)/shard_map/cond/branch_1_fun/dot_general | solution.py:51
  103.5 0.3 copy.28
  103.7 0.9 copy-done.1
  (40 shorter events, 0.6 us)
Async XLA Ops:
  0.0 10.2 %copy-start = (f32[4,32,1440]{2,1,0:T(8,128)S(1)}, f32[4,32,1440]{2,1,0:T(8,128)}, u32[]{:S(2)}) copy-start(f32[4,32,1440]{2,1,0:T(8,128)} %param.9) | copy-start | bytes 2211844
  0.0 10.6 %copy-start.2 = (f32[4,32,1440]{2,1,0:T(8,128)S(1)}, f32[4,32,1440]{2,1,0:T(8,128)}, u32[]{:S(2)}) copy-start(f32[4,32,1440]{2,1,0:T(8,128)} %param.10) | copy-start | bytes 2211844
  2.8 79.7 %collective-permute-start = (f32[2,2,32,1440]{3,2,1,0:T(8,128)}, f32[2,2,32,1440]{3,2,1,0:T(8,128)}, u32[]{:S(2)}, u32[]{:S(2)}) collective-permute-start(f32[2,2,32,1440]{3,2,1,0:T(8,128)} %get-tuple-element.115), channel_id=1, source_target_pairs={{0,1},{1,2},{2,3},{3,4},{4,5},{5,6},{6,7},{7,8},{8,9},{9,10},{10,1... | collective-permute-start | bytes 2211848 | tf_op jit(solution)/shard_map/ppermute | solution.py:15
  6.0 76.5 %collective-permute-start.1 = (f32[2,2,32,1440]{3,2,1,0:T(8,128)}, f32[2,2,32,1440]{3,2,1,0:T(8,128)}, u32[]{:S(2)}, u32[]{:S(2)}) collective-permute-start(f32[2,2,32,1440]{3,2,1,0:T(8,128)} %get-tuple-element.116), channel_id=1, source_target_pairs={{1,0},{2,1},{3,2},{4,3},{5,4},{6,5},{7,6},{8,7},{9,8},{10,9},{11,1... | collective-permute-start | bytes 2211848 | tf_op jit(solution)/shard_map/ppermute | solution.py:17
  12.5 19.6 %copy-start.7 = (f32[32]{0:T(128)S(1)}, f32[32]{0:T(128)}, u32[]{:S(2)}) copy-start(f32[32]{0:T(128)} %param.12) | copy-start | bytes 388
  12.5 19.6 %copy-start.3 = (f32[4,32,1440]{2,1,0:T(8,128)S(1)}, f32[4,32,1440]{2,1,0:T(8,128)}, u32[]{:S(2)}) copy-start(f32[4,32,1440]{2,1,0:T(8,128)} %param.10) | copy-start | bytes 2211844
  12.5 19.6 %slice-start = ((f32[4,32,1440]{2,1,0:T(8,128)}), f32[4,32,1]{2,1,0:T(8,128)S(1)}, s32[]{:S(2)}) async-start(f32[4,32,1440]{2,1,0:T(8,128)} %param.10), calls=%async_computation | async-start | bytes 131072 | tf_op jit(solution)/shard_map/jit(_roll_static)/slice | solution.py:107
  12.5 19.6 %copy-start.5 = (f32[32]{0:T(128)S(1)}, f32[32]{0:T(128)}, u32[]{:S(2)}) copy-start(f32[32]{0:T(128)} %param.13) | copy-start | bytes 388
  32.1 2.7 %copy-start.9 = (u32[32]{0:T(128)S(1)}, u32[32]{0:T(128)}, u32[]{:S(2)}) copy-start(u32[32]{0:T(128)} %constant.95) | copy-start | bytes 388
  32.1 40.2 %copy-start.6 = (s32[64]{0:T(128)S(1)}, s32[64]{0:T(128)}, u32[]{:S(2)}) copy-start(s32[64]{0:T(128)} %param.14) | copy-start | bytes 772
  32.1 41.0 %copy-start.8 = (s32[64]{0:T(128)S(1)}, s32[64]{0:T(128)}, u32[]{:S(2)}) copy-start(s32[64]{0:T(128)} %param.15) | copy-start | bytes 772
  74.3 8.2 %copy-start.4 = (f32[4,32,1440]{2,1,0:T(8,128)S(1)}, f32[4,32,1440]{2,1,0:T(8,128)}, u32[]{:S(2)}) copy-start(f32[4,32,1440]{2,1,0:T(8,128)} %param.11) | copy-start | bytes 2211844
  103.7 0.9 copy-start.1
